TPU v7x, 32 devices: a whole 2x2x4 slice. The times are simulated.
32 devices in a mesh: shard: 8 (over z, core), rep: 4 (over y, x).
Axes of the slice: x: 2, y: 2, z: 4, core: 2. Of those that a mesh axis runs over, the one named last changes fastest.
Arguments:
- tokens: bfloat16 [12288, 5120], P(('shard', 'rep')), may hold values from -700 to 700
- norm_gain: float32 [5120], replicated, may hold values from 0.1 to 1.9
- key_bias: float32 [1024], replicated, may hold values from -4 to 4
- key_weight: bfloat16 [8192, 1024], P('shard'), may hold values from -0.078125 to 0.078125
- cotangent: bfloat16 [12288, 1024], P(('shard', 'rep')), may hold values from -40 to 40
- block_slot: int32 [40], replicated, may hold values from 0 to 63, as said below
Outputs:
- projected: bfloat16 [12288, 1024], P(('shard', 'rep'))
- token_grad: bfloat16 [12288, 5120], P(('shard', 'rep'))
- weight_grad: float32 [8192, 1024], P('shard')
- gain_grad: float32 [5120], replicated
- bias_grad: float32 [1024], replicated
Inputs may be any that keep to these rules, and one draw needn't show every extreme that they name: Entries are distinct; block b lies on the device of shard with index block_slot[b] // 8, at its local slot block_slot[b] % 8; in every draw some device holds 8 blocks.
All inputs are finite; a program needn't handle non-finite values.
Results may differ from a plain program's by a relative error of at most 0.013.
Values may be sent and summed in bfloat16 or wider, within the bound.
A program may use at most 128 MiB of HBM per device.

v0:
```python
import jax
import jax.numpy as jnp
from jax import lax
from jax.sharding import PartitionSpec as P

BLK = 128
EPS = 1e-06


def normalize(tokens, norm_gain):
    values = tokens.astype(jnp.float32)
    inv_rms = lax.rsqrt(jnp.mean(values * values, axis=-1, keepdims=True) + EPS)
    normed = (values * inv_rms * norm_gain).astype(jnp.bfloat16)
    return (values, inv_rms, normed)


def token_backward(values, inv_rms, grad_normed, norm_gain):
    scaled = grad_normed * norm_gain
    inner = jnp.mean(scaled * values, axis=-1, keepdims=True)
    return (inv_rms * (scaled - values * inv_rms * inv_rms * inner)).astype(jnp.bfloat16)


def local(tokens, norm_gain, key_bias, key_weight, cotangent, block_slot):
    values, inv_rms, normed = normalize(tokens, norm_gain)
    row_count = tokens.shape[0]
    width = tokens.shape[1]
    local_rows = key_weight.shape[0]
    shard_count = lax.axis_size("shard")
    replicas = lax.axis_size("rep")
    slot_total = shard_count * local_rows // BLK
    block_count = width // BLK
    block_of_slot = (
        jnp.full((slot_total,), -1, jnp.int32)
        .at[block_slot]
        .set(jnp.arange(block_count, dtype=jnp.int32))
    )
    present = block_of_slot >= 0
    normed_blocks = normed.reshape(row_count, block_count, BLK)
    normed_slots = jnp.take(normed_blocks, jnp.maximum(block_of_slot, 0), axis=1)
    normed_slots = jnp.where(present[None, :, None], normed_slots, jnp.zeros((), jnp.bfloat16))
    normed_slots = normed_slots.reshape(row_count, slot_total * BLK)
    piece = lax.all_gather(key_weight, "shard", axis=0, tiled=True)
    columns = normed_slots
    forward_sum = jnp.dot(columns, piece, preferred_element_type=jnp.float32)
    backward_part = lax.dot_general(
        cotangent, piece, (((1,), (1,)), ((), ())), preferred_element_type=jnp.float32
    )
    projected = (forward_sum + key_bias).astype(jnp.bfloat16)
    grad_normed = jnp.take(backward_part.reshape(row_count, slot_total, BLK), block_slot, axis=1)
    grad_normed = grad_normed.reshape(row_count, width)
    token_grad = token_backward(values, inv_rms, grad_normed, norm_gain)
    grad_scale = float(row_count * shard_count * replicas) ** (-0.5)
    columns = normed_slots
    group_sum = lax.psum_scatter(
        (
            lax.dot_general(
                columns, cotangent, (((0,), (0,)), ((), ())), preferred_element_type=jnp.float32
            )
            * grad_scale
        ).astype(jnp.bfloat16),
        "shard",
        scatter_dimension=0,
        tiled=True,
    ).astype(jnp.float32)
    gain_part = jnp.sum(grad_normed * values * inv_rms, axis=0) * grad_scale
    bias_part = jnp.sum(cotangent.astype(jnp.float32), axis=0) * grad_scale
    weight_grad = lax.psum(group_sum, "rep")
    gain_grad, bias_grad = lax.psum((gain_part, bias_part), ("shard", "rep"))
    return (projected, token_grad, weight_grad, gain_grad, bias_grad)


def solution(mesh):
    return jax.shard_map(
        local,
        mesh=mesh,
        in_specs=(
            P(("shard", "rep"), None),
            P(),
            P(),
            P("shard", None),
            P(("shard", "rep"), None),
            P(),
        ),
        out_specs=(
            P(("shard", "rep"), None),
            P(("shard", "rep"), None),
            P("shard", None),
            P(),
            P(),
        ),
        check_vma=False,
    )
```

profile of v0, /device:TPU:16, one launch (start us, length us, event | category | flops | bytes accessed | tf_op | source)
XLA Modules:
  0.0 578.5 jit_solution(7815864115164983269)
XLA Ops:
  7.2 0.0 copy-start.6
  7.2 0.0 copy-start.3
  7.2 0.0 all-gather.2.cloned.1.call-start
  7.2 0.7 all-gather.2.cloned.1.call-update
  7.9 0.0 reduce-scatter.2.cloned.1.call-start
  8.0 6.3 %copy.12 = bf16[384,5120]{0,1:T(8,128)(2,1)} copy(bf16[384,5120]{1,0:T(8,128)(2,1)} %param.6) | data formatting | bytes 7864320 | tf_op args[0]
  14.2 0.0 copy-done.6
  14.2 0.7 scatter_custom_fusion
  15.0 3.0 fusion.7
  18.1 0.1 broadcast_bitcast_fusion.2
  18.1 0.1 broadcast_bitcast_fusion
  18.2 141.7 %all-gather.2.cloned.1.call-done = bf16[8192,1024]{1,0:T(8,128)(2,1)} async-done(((bf16[1024,1024]{1,0:T(8,128)(2,1)}), bf16[8192,1024]{1,0:T(8,128)(2,1)}) %all-gather.2.cloned.1.call-update) | async-done | bytes 16777232 | tf_op jit(solution)/shard_map/all_gather | solution.py:42
  160.0 12.9 %convolution_bitcast_fusion = f32[48,64,8,128]{3,2,1,0:T(8,128)} fusion(bf16[384,1024]{1,0:T(8,128)(2,1)S(1)} %copy-done.3, bf16[8192,1024]{1,0:T(8,128)(2,1)} %all-gather.2.cloned.1.call-done), kind=kOutput, calls=%fused_computation.24 | convolution fusion | flops 6442450944 | bytes 30146560 | tf_op jit(solution)/shard_map/dot_general | solution.py:45
  172.9 10.8 %copy.20 = f32[48,64,8,128]{3,2,0,1:T(8,128)} copy(f32[48,64,8,128]{3,2,1,0:T(8,128)} %convolution_bitcast_fusion) | data formatting | bytes 25165824 | tf_op jit(solution)/shard_map/reshape | solution.py:49
  183.7 8.7 %gather_fusion.1 = f32[40,384,128]{2,1,0:T(8,128)} fusion(f32[384,64,128]{2,0,1:T(8,128)} %bitcast.34, s32[1024]{0:T(1024)S(1)} %pad_clamp_fusion), kind=kCustom, calls=%fused_computation.1 | custom fusion | bytes 15728800 | tf_op jit(solution)/shard_map/jit(_take)/gather | solution.py:49
  192.4 9.1 %copy.16 = f32[384,40,128]{0,2,1:T(8,128)} copy(f32[384,40,128]{2,0,1:T(8,128)} %bitcast.35) | data formatting | bytes 15728640 | tf_op jit(solution)/shard_map/jit(_take)/gather | solution.py:49
  201.5 8.8 %fusion.10 = (f32[5120]{0:T(1024)S(1)}, f32[384]{0:T(512)S(1)}) fusion(bf16[384,5120]{0,1:T(8,128)(2,1)} %copy.12, f32[384,40,128]{0,2,1:T(8,128)} %copy.16, f32[384]{0:T(512)S(1)} %add_rsqrt_fusion, pred[5120]{0:T(1024)(128)(4,1)S(1)} %broadcast_bitcast_fusion.2, f32[5120]{0:T(1024)S(1)} %copy-done.4), kind=kLoop, calls=%fused_computation.19 | loop fusion | flops 15723136 | bytes 11845632 | tf_op jit(solution)/shard_map/reduce_sum | solution.py:65
  210.3 5.5 fusion.6
  215.8 6.3 %copy.13 = bf16[384,40,128]{2,0,1:T(8,128)(2,1)} copy(bf16[384,40,128]{0,2,1:T(8,128)(2,1)} %bitcast.37) | data formatting | bytes 7864320 | tf_op jit(solution)/shard_map/reshape | solution.py:38
  222.1 6.1 %gather_fusion = bf16[64,384,128]{2,1,0:T(8,128)(2,1)} fusion(bf16[384,40,128]{2,0,1:T(8,128)(2,1)} %copy.13, s32[1024]{0:T(1024)S(1)} %pad_clamp_fusion.1), kind=kCustom, calls=%fused_computation | custom fusion | bytes 12583168 | tf_op jit(solution)/shard_map/jit(_take)/gather | solution.py:39
  228.2 8.6 %copy.14 = bf16[384,64,128]{0,2,1:T(8,128)(2,1)} copy(bf16[384,64,128]{2,0,1:T(8,128)(2,1)} %bitcast.36) | data formatting | bytes 12582912 | tf_op jit(solution)/shard_map/jit(_take)/gather | solution.py:39
  236.8 6.9 %fusion.12 = bf16[384,8192]{0,1:T(8,128)(2,1)S(1)} fusion(bf16[384,64,128]{0,2,1:T(8,128)(2,1)} %copy.14, pred[8192]{0:T(1024)(128)(4,1)S(1)} %get-tuple-element.18, pred[8192]{0:T(1024)(128)(4,1)S(1)} %get-tuple-element.19), kind=kLoop, calls=%fused_computation.23 | loop fusion | flops 6291456 | bytes 12599296 | tf_op jit(solution)/shard_map/jit(_where)/select_n | solution.py:40
  243.7 2.6 copy-done.2
  246.3 11.7 %multiply_convert_fusion = bf16[8192,1024]{1,0:T(8,128)(2,1)} fusion(bf16[384,8192]{0,1:T(8,128)(2,1)S(1)} %fusion.12, bf16[384,1024]{1,0:T(8,128)(2,1)S(1)} %copy-done.3), kind=kOutput, calls=%fused_computation.3 | convolution fusion | flops 6459228160 | bytes 23855104 | tf_op jit(solution)/shard_map/dot_general | solution.py:56
  258.0 0.0 reduce-scatter.2.cloned.1.call-update
  258.0 0.0 copy-start.5
  258.0 0.1 convert_reduce_fusion
  258.2 6.3 %copy.17 = bf16[384,5120]{1,0:T(8,128)(2,1)} copy(bf16[384,5120]{0,1:T(8,128)(2,1)} %get-tuple-element.14) | data formatting | bytes 7864320
  264.4 42.3 %all-reduce = (f32[5120]{0:T(1024)}, f32[1024]{0:T(1024)}) all-reduce(f32[5120]{0:T(1024)S(1)} %broadcast_multiply_fusion, f32[1024]{0:T(1024)S(1)} %broadcast_multiply_fusion.1), channel_id=1, replica_groups=mesh['shard'=8,'rep'=4] {'shard','rep'}, use_global_device_ids=true, to_apply=%region_6.7 | all-reduce | flops 6144 | bytes 49152 | tf_op jit(solution)/shard_map/psum | solution.py:68
  306.7 13.0 %add_convert_fusion = bf16[384,1024]{1,0:T(8,128)(2,1)} fusion(bf16[384,8192]{0,1:T(8,128)(2,1)} %copy-done.2, bf16[8192,1024]{1,0:T(8,128)(2,1)} %all-gather.2.cloned.1.call-done, f32[1024]{0:T(1024)S(1)} %copy-done.5), kind=kOutput, calls=%fused_computation.26 | convolution fusion | flops 6443237376 | bytes 23859200 | tf_op jit(solution)/shard_map/dot_general | solution.py:44
  319.7 105.2 %reduce-scatter.2.cloned.1.call-done = bf16[1024,1024]{1,0:T(8,128)(2,1)} async-done(((bf16[8192,1024]{1,0:T(8,128)(2,1)}), bf16[1024,1024]{1,0:T(8,128)(2,1)}) %reduce-scatter.2.cloned.1.call-update) | async-done | bytes 2097168 | tf_op jit(solution)/shard_map/reduce_scatter | solution.py:54
  424.9 146.8 %all-reduce.2 = f32[1024,1024]{1,0:T(8,128)} all-reduce(bf16[1024,1024]{1,0:T(8,128)(2,1)} %reduce-scatter.2.cloned.1.call-done), channel_id=1, replica_groups=mesh['shard'=8,'rep'=4] {'rep'}, use_global_device_ids=true, to_apply=%region_4.5 | all-reduce | flops 1048576 | bytes 6291456 | tf_op jit(solution)/shard_map/psum | solution.py:67
  (20 shorter events, 0.1 us)
Async XLA Ops:
  7.2 7.1 %copy-start.6 = (s32[40]{0:T(128)S(1)}, s32[40]{0:T(128)}, u32[]{:S(2)}) copy-start(s32[40]{0:T(128)} %param.11) | copy-start | bytes 484
  7.2 152.8 %copy-start.3 = (bf16[384,1024]{1,0:T(8,128)(2,1)S(1)}, bf16[384,1024]{1,0:T(8,128)(2,1)}, u32[]{:S(2)}) copy-start(bf16[384,1024]{1,0:T(8,128)(2,1)} %param.10) | copy-start | bytes 2359300
  7.2 152.8 %all-gather.2.cloned.1.call-start = ((), (), s32[]{:S(2)}) async-start(), calls=%async_computation.1 | async-start | bytes 18874368 | tf_op jit(solution)/shard_map/all_gather | solution.py:42
  7.9 417.0 %reduce-scatter.2.cloned.1.call-start = ((), (), s32[]{:S(2)}) async-start(), calls=%async_computation.2 | async-start | bytes 18874368 | tf_op jit(solution)/shard_map/reduce_scatter | solution.py:54
  192.4 9.1 %copy-start.4 = (f32[5120]{0:T(1024)S(1)}, f32[5120]{0:T(1024)}, u32[]{:S(2)}) copy-start(f32[5120]{0:T(1024)} %param.7) | copy-start | bytes 61444
  201.5 8.8 %copy-start = (f32[384,40,128]{0,2,1:T(8,128)S(1)}, f32[384,40,128]{0,2,1:T(8,128)}, u32[]{:S(2)}) copy-start(f32[384,40,128]{0,2,1:T(8,128)} %copy.16) | copy-start | bytes 23592964
  201.5 8.8 %copy-start.1 = (bf16[384,5120]{0,1:T(8,128)(2,1)S(1)}, bf16[384,5120]{0,1:T(8,128)(2,1)}, u32[]{:S(2)}) copy-start(bf16[384,5120]{0,1:T(8,128)(2,1)} %copy.12) | copy-start | bytes 11796484
  243.7 2.6 copy-start.2
  258.0 48.7 %copy-start.5 = (f32[1024]{0:T(1024)S(1)}, f32[1024]{0:T(1024)}, u32[]{:S(2)}) copy-start(f32[1024]{0:T(1024)} %param.8) | copy-start | bytes 12292
Sparse Core Ops, SparseCore 0:
  9.6 150.3 all-gather.1
  258.1 166.7 reduce-scatter.1
where the time goes:
time: 580 us; the launch traced here: 579 us
  waiting for transfers between devices  248 us (43%)
  blocking collectives  189 us (33%)
  local copies, waits for them, and re-layouts  65.7 us (11%)
  matrix products  37.5 us (6%)
  other arithmetic  24.4 us (4%)
  between operations  14.2 us (2%)
    psum x1, blocking collectives, local(): weight_grad = lax.psum(group_sum, 'rep')  147 us
    all_gather x1, waiting for transfers between devices, local(): piece = lax.all_gather(key_weight, 'shard', axis=0, tiled=True)  142 us
    reduce_scatter x1, waiting for transfers between devices, local(): lax.psum_scatter((lax.dot_general(columns, cotangent, (((0,), (0,)), ((),...  105 us
    psum x1, blocking collectives, local(): gain_grad, bias_grad = lax.psum((gain_part, bias_part), ('shard', 'rep'))  42.3 us
    gather x2, local copies, waits for them, and re-layouts, local(): jnp.take(backward_part.reshape(row_count, slot_total, BLK), block_slot, a...  17.8 us
    unnamed x16, local copies, waits for them, and re-layouts  15.2 us
    gather x2, local copies, waits for them, and re-layouts, local(): jnp.take(normed_blocks, jnp.maximum(block_of_slot, 0), axis=1)  14.7 us
    dot_general x1, matrix products, local(): forward_sum = jnp.dot(columns, piece, preferred_element_type=jnp.float32)  13 us
  transfers between devices with their start and end apart: 2, of which 2 were waited for; matrix products, arithmetic and copies ran while one was open for 5% of the time, Pallas kernels for 0%

commit v1 on v0

--- a/solution.py
+++ b/solution.py
@@ -39,7 +39,14 @@
     normed_slots = jnp.take(normed_blocks, jnp.maximum(block_of_slot, 0), axis=1)
     normed_slots = jnp.where(present[None, :, None], normed_slots, jnp.zeros((), jnp.bfloat16))
     normed_slots = normed_slots.reshape(row_count, slot_total * BLK)
-    piece = lax.all_gather(key_weight, "shard", axis=0, tiled=True)
+    ring = [key_weight]
+    for hop in range(7):
+        ring.append(lax.ppermute(ring[-1], "shard", [(dev, (dev + 1) % 8) for dev in range(8)]))
+    piece = jnp.roll(
+        jnp.concatenate(ring[::-1], axis=0),
+        (lax.axis_index("shard") + 1) * ring[0].shape[0],
+        axis=0,
+    )
     columns = normed_slots
     forward_sum = jnp.dot(columns, piece, preferred_element_type=jnp.float32)
     backward_part = lax.dot_general(

time: 580 us -> 633 us (1.091)
  waiting for transfers between devices: 248 us -> 273 us
  local copies, waits for them, and re-layouts: 65.7 us -> 81.7 us
  blocking collectives: 189 us -> 200 us
    ppermute x0 -> x7, waiting for transfers between devices: none -> 168 us  [local(): lax.ppermute(ring[-1], 'shard', [(dev, (dev + 1) % 8) for dev in range(8)])]
    all_gather x1 -> x0, waiting for transfers between devices: 142 us -> none  [local(): piece = lax.all_gather(key_weight, 'shard', axis=0, tiled=True)]
    unnamed x16 -> x49, local copies, waits for them, and re-layouts: 15.2 us -> 49.7 us
    reshape x1 -> x0, local copies, waits for them, and re-layouts: 10.8 us -> none  [local(): backward_part.reshape(row_count, slot_total, BLK)]
    psum x1, blocking collectives: 42.3 us -> 52.8 us  [local(): gain_grad, bias_grad = lax.psum((gain_part, bias_part), ('shard', 'rep'))]
    gather x2 -> x1, local copies, waits for them, and re-layouts: 17.8 us -> 8.71 us  [local(): jnp.take(backward_part.reshape(row_count, slot_total, BLK), block_slot, a...]
  transfers between devices with their start and end apart: 2 -> 8, of which waited for: 2 -> 8; matrix products, arithmetic and copies ran while one was open for 5% -> 5% of each run, Pallas kernels for 0% -> 0%
where the time goes in v1:
time: 633 us; the launch traced here: 632 us
  waiting for transfers between devices  273 us (43%)
  blocking collectives  200 us (32%)
  local copies, waits for them, and re-layouts  81.7 us (13%)
  matrix products  39.7 us (6%)
  other arithmetic  23.6 us (4%)
  between operations  14.2 us (2%)
    ppermute x7, waiting for transfers between devices, local(): lax.ppermute(ring[-1], 'shard', [(dev, (dev + 1) % 8) for dev in range(8)])  168 us
    psum x1, blocking collectives, local(): weight_grad = lax.psum(group_sum, 'rep')  147 us
    reduce_scatter x1, waiting for transfers between devices, local(): lax.psum_scatter((lax.dot_general(columns, cotangent, (((0,), (0,)), ((),...  105 us
    psum x1, blocking collectives, local(): gain_grad, bias_grad = lax.psum((gain_part, bias_part), ('shard', 'rep'))  52.8 us
    unnamed x49, local copies, waits for them, and re-layouts  49.7 us
    dot_general x1, matrix products, local(): lax.dot_general(cotangent, piece, (((1,), (1,)), ((), ())), preferred_ele...  15.1 us
    gather x2, local copies, waits for them, and re-layouts, local(): jnp.take(normed_blocks, jnp.maximum(block_of_slot, 0), axis=1)  14.7 us
    dot_general x1, matrix products, local(): forward_sum = jnp.dot(columns, piece, preferred_element_type=jnp.float32)  13 us
  transfers between devices with their start and end apart: 8, of which 8 were waited for; matrix products, arithmetic and copies ran while one was open for 5% of the time, Pallas kernels for 0%

profile of v1, /device:TPU:16, one launch (start us, length us, event | category | flops | bytes accessed | tf_op | source)
XLA Modules:
  0.0 632.4 jit_solution(74251185136835088)
XLA Ops:
  7.3 25.7 %collective-permute-done = bf16[1024,1024]{1,0:T(8,128)(2,1)S(1)} collective-permute-done((bf16[1024,1024]{1,0:T(8,128)(2,1)}, bf16[1024,1024]{1,0:T(8,128)(2,1)S(1)}, u32[]{:S(2)}, u32[]{:S(2)}) %collective-permute-start) | collective-permute-done | bytes 2097184 | tf_op jit(solution)/shard_map/ppermute | solution.py:44
  32.9 25.5 %collective-permute-done.1 = bf16[1024,1024]{1,0:T(8,128)(2,1)S(1)} collective-permute-done((bf16[1024,1024]{1,0:T(8,128)(2,1)S(1)}, bf16[1024,1024]{1,0:T(8,128)(2,1)S(1)}, u32[]{:S(2)}, u32[]{:S(2)}) %collective-permute-start.1) | collective-permute-done | bytes 2097184 | tf_op jit(solution)/shard_map/ppermute | solution.py:44
  59.7 25.5 %collective-permute-done.2 = bf16[1024,1024]{1,0:T(8,128)(2,1)S(1)} collective-permute-done((bf16[1024,1024]{1,0:T(8,128)(2,1)S(1)}, bf16[1024,1024]{1,0:T(8,128)(2,1)S(1)}, u32[]{:S(2)}, u32[]{:S(2)}) %collective-permute-start.2) | collective-permute-done | bytes 2097184 | tf_op jit(solution)/shard_map/ppermute | solution.py:44
  86.5 25.5 %collective-permute-done.3 = bf16[1024,1024]{1,0:T(8,128)(2,1)S(1)} collective-permute-done((bf16[1024,1024]{1,0:T(8,128)(2,1)S(1)}, bf16[1024,1024]{1,0:T(8,128)(2,1)S(1)}, u32[]{:S(2)}, u32[]{:S(2)}) %collective-permute-start.3) | collective-permute-done | bytes 2097184 | tf_op jit(solution)/shard_map/ppermute | solution.py:44
  113.3 25.5 %collective-permute-done.4 = bf16[1024,1024]{1,0:T(8,128)(2,1)S(1)} collective-permute-done((bf16[1024,1024]{1,0:T(8,128)(2,1)S(1)}, bf16[1024,1024]{1,0:T(8,128)(2,1)S(1)}, u32[]{:S(2)}, u32[]{:S(2)}) %collective-permute-start.4) | collective-permute-done | bytes 2097184 | tf_op jit(solution)/shard_map/ppermute | solution.py:44
  140.1 25.6 %collective-permute-done.5 = bf16[1024,1024]{1,0:T(8,128)(2,1)} collective-permute-done((bf16[1024,1024]{1,0:T(8,128)(2,1)S(1)}, bf16[1024,1024]{1,0:T(8,128)(2,1)}, u32[]{:S(2)}, u32[]{:S(2)}) %collective-permute-start.5) | collective-permute-done | bytes 2097184 | tf_op jit(solution)/shard_map/ppermute | solution.py:44
  165.6 6.3 copy.13
  172.7 3.2 fusion.11
  176.1 15.3 %collective-permute-done.6 = bf16[1024,1024]{1,0:T(8,128)(2,1)} collective-permute-done((bf16[1024,1024]{1,0:T(8,128)(2,1)}, bf16[1024,1024]{1,0:T(8,128)(2,1)}, u32[]{:S(2)}, u32[]{:S(2)}) %collective-permute-start.6) | collective-permute-done | bytes 2097184 | tf_op jit(solution)/shard_map/ppermute | solution.py:44
  191.4 3.1 constant_dynamic-update-slice_fusion.15
  194.5 3.2 constant_dynamic-update-slice_fusion.14
  199.2 1.5 constant_dynamic-update-slice_fusion.12
  200.8 1.5 constant_dynamic-update-slice_fusion.11
  206.8 3.1 constant_dynamic-update-slice_fusion.7
  209.9 3.1 constant_dynamic-update-slice_fusion.6
  214.4 1.5 constant_dynamic-update-slice_fusion.4
  216.0 1.5 constant_dynamic-update-slice_fusion.3
  222.0 15.1 %fusion = f32[8192,384]{1,0:T(8,128)} fusion(bf16[384,1024]{1,0:T(8,128)(2,1)S(1)} %copy-done.12, bf16[16384,1024]{1,0:T(8,128)(2,1)} %constant_dynamic-update-slice_fusion, s32[]{:T(128)S(6)} %select_n.41), kind=kOutput, calls=%fused_computation.4 | convolution fusion | flops 6442450944 | bytes 30146564 | tf_op jit(solution)/shard_map/dot_general | solution.py:52
  237.0 8.7 %gather_fusion.1 = f32[40,384,128]{1,2,0:T(8,128)} fusion(f32[384,64,128]{0,2,1:T(8,128)} %bitcast.33, s32[1024]{0:T(1024)S(1)} %get-tuple-element.18), kind=kCustom, calls=%fused_computation.1 | custom fusion | bytes 15728800 | tf_op jit(solution)/shard_map/jit(_take)/gather | solution.py:56
  245.8 7.8 %fusion.14 = (f32[5120]{0:T(1024)S(1)}, f32[384]{0:T(512)S(1)}) fusion(bf16[384,5120]{0,1:T(8,128)(2,1)} %copy.13, f32[40,384,128]{1,2,0:T(8,128)} %gather_fusion.1, f32[384]{0:T(512)S(1)} %add_rsqrt_fusion, pred[5120]{0:T(1024)(128)(4,1)S(1)} %broadcast_bitcast_fusion.2, f32[5120]{0:T(1024)S(1)} %copy-done.13), kind=kLoop, calls=%fused_computation.22 | loop fusion | flops 15723136 | bytes 11845632 | tf_op jit(solution)/shard_map/reduce_sum | solution.py:72
  253.6 5.5 fusion.10
  259.1 6.3 copy.14
  265.4 6.1 gather_fusion
  271.4 8.6 %copy.15 = bf16[384,64,128]{0,2,1:T(8,128)(2,1)} copy(bf16[384,64,128]{2,0,1:T(8,128)(2,1)} %bitcast.31) | data formatting | bytes 12582912 | tf_op jit(solution)/shard_map/jit(_take)/gather | solution.py:39
  280.1 6.9 %fusion.16 = bf16[384,8192]{0,1:T(8,128)(2,1)S(1)} fusion(bf16[384,64,128]{0,2,1:T(8,128)(2,1)} %copy.15, pred[8192]{0:T(1024)(128)(4,1)S(1)} %get-tuple-element.20, pred[8192]{0:T(1024)(128)(4,1)S(1)} %get-tuple-element.21), kind=kLoop, calls=%fused_computation.26 | loop fusion | flops 6291456 | bytes 12599296 | tf_op jit(solution)/shard_map/jit(_where)/select_n | solution.py:40
  287.0 2.6 copy-done.11
  289.6 11.7 %multiply_convert_fusion = bf16[8192,1024]{1,0:T(8,128)(2,1)} fusion(bf16[384,8192]{0,1:T(8,128)(2,1)S(1)} %fusion.16, bf16[384,1024]{1,0:T(8,128)(2,1)S(1)} %copy-done.12), kind=kOutput, calls=%fused_computation.3 | convolution fusion | flops 6459228160 | bytes 23855104 | tf_op jit(solution)/shard_map/dot_general | solution.py:63
  301.4 6.5 %copy.16 = bf16[384,5120]{1,0:T(8,128)(2,1)} copy(bf16[384,5120]{0,1:T(8,128)(2,1)} %get-tuple-element.14) | data formatting | bytes 7864320
  307.9 52.8 %all-reduce = (f32[5120]{0:T(1024)}, f32[1024]{0:T(1024)}) all-reduce(f32[5120]{0:T(1024)S(1)} %broadcast_multiply_fusion, f32[1024]{0:T(1024)S(1)} %broadcast_multiply_fusion.1), channel_id=1, replica_groups=mesh['shard'=8,'rep'=4] {'shard','rep'}, use_global_device_ids=true, to_apply=%region_6.7 | all-reduce | flops 6144 | bytes 49152 | tf_op jit(solution)/shard_map/psum | solution.py:75
  360.7 13.0 %add_convert_fusion = bf16[384,1024]{1,0:T(8,128)(2,1)} fusion(bf16[384,8192]{0,1:T(8,128)(2,1)} %copy-done.11, bf16[16384,1024]{1,0:T(8,128)(2,1)} %constant_dynamic-update-slice_fusion, s32[]{:T(128)S(6)} %select_n.41, f32[1024]{0:T(1024)S(1)} %copy-done.14), kind=kOutput, calls=%fused_computation.28 | convolution fusion | flops 6443237376 | bytes 23859204 | tf_op jit(solution)/shard_map/dot_general | solution.py:51
  373.7 105.0 %reduce-scatter.2.cloned.1.call-done = bf16[1024,1024]{1,0:T(8,128)(2,1)} async-done(((bf16[8192,1024]{1,0:T(8,128)(2,1)}), bf16[1024,1024]{1,0:T(8,128)(2,1)}) %reduce-scatter.2.cloned.1.call-update) | async-done | bytes 2097168 | tf_op jit(solution)/shard_map/reduce_scatter | solution.py:61
  478.8 146.8 %all-reduce.2 = f32[1024,1024]{1,0:T(8,128)} all-reduce(bf16[1024,1024]{1,0:T(8,128)(2,1)} %reduce-scatter.2.cloned.1.call-done), channel_id=1, replica_groups=mesh['shard'=8,'rep'=4] {'rep'}, use_global_device_ids=true, to_apply=%region_4.5 | all-reduce | flops 1048576 | bytes 6291456 | tf_op jit(solution)/shard_map/psum | solution.py:74
  (62 shorter events, 18.4 us)
Async XLA Ops:
  7.2 164.7 %copy-start.15 = (s32[40]{0:T(128)S(1)}, s32[40]{0:T(128)}, u32[]{:S(2)}) copy-start(s32[40]{0:T(128)} %param.11) | copy-start | bytes 484
  7.2 471.6 %reduce-scatter.2.cloned.1.call-start = ((), (), s32[]{:S(2)}) async-start(), calls=%async_computation.1 | async-start | bytes 18874368 | tf_op jit(solution)/shard_map/reduce_scatter | solution.py:61
  7.2 25.7 %collective-permute-start = (bf16[1024,1024]{1,0:T(8,128)(2,1)}, bf16[1024,1024]{1,0:T(8,128)(2,1)S(1)}, u32[]{:S(2)}, u32[]{:S(2)}) collective-permute-start(bf16[1024,1024]{1,0:T(8,128)(2,1)} %param.9), channel_id=1, source_target_pairs={{0,4},{4,8},{8,12},{12,16},{16,20},{20,24},{24,28},{28,0},{1,5},{5... | collective-permute-start | bytes 6291464 | tf_op jit(solution)/shard_map/ppermute | solution.py:44
  32.9 25.5 %collective-permute-start.1 = (bf16[1024,1024]{1,0:T(8,128)(2,1)S(1)}, bf16[1024,1024]{1,0:T(8,128)(2,1)S(1)}, u32[]{:S(2)}, u32[]{:S(2)}) collective-permute-start(bf16[1024,1024]{1,0:T(8,128)(2,1)S(1)} %collective-permute-done), channel_id=1, source_target_pairs={{0,4},{4,8},{8,12},{12,16},{16,20},{20,24},{24,28},{28,0},{1,5},{5... | collective-permute-start | bytes 6291464 | tf_op jit(solution)/shard_map/ppermute | solution.py:44
  58.4 1.3 copy-start.3
  59.7 25.5 %collective-permute-start.2 = (bf16[1024,1024]{1,0:T(8,128)(2,1)S(1)}, bf16[1024,1024]{1,0:T(8,128)(2,1)S(1)}, u32[]{:S(2)}, u32[]{:S(2)}) collective-permute-start(bf16[1024,1024]{1,0:T(8,128)(2,1)S(1)} %collective-permute-done.1), channel_id=1, source_target_pairs={{0,4},{4,8},{8,12},{12,16},{16,20},{20,24},{24,28},{28,0},{1,5},{5... | collective-permute-start | bytes 6291464 | tf_op jit(solution)/shard_map/ppermute | solution.py:44
  85.2 1.3 copy-start.5
  86.5 25.5 %collective-permute-start.3 = (bf16[1024,1024]{1,0:T(8,128)(2,1)S(1)}, bf16[1024,1024]{1,0:T(8,128)(2,1)S(1)}, u32[]{:S(2)}, u32[]{:S(2)}) collective-permute-start(bf16[1024,1024]{1,0:T(8,128)(2,1)S(1)} %collective-permute-done.2), channel_id=1, source_target_pairs={{0,4},{4,8},{8,12},{12,16},{16,20},{20,24},{24,28},{28,0},{1,5},{5... | collective-permute-start | bytes 6291464 | tf_op jit(solution)/shard_map/ppermute | solution.py:44
  111.9 1.4 copy-start.7
  113.3 25.5 %collective-permute-start.4 = (bf16[1024,1024]{1,0:T(8,128)(2,1)S(1)}, bf16[1024,1024]{1,0:T(8,128)(2,1)S(1)}, u32[]{:S(2)}, u32[]{:S(2)}) collective-permute-start(bf16[1024,1024]{1,0:T(8,128)(2,1)S(1)} %collective-permute-done.3), channel_id=1, source_target_pairs={{0,4},{4,8},{8,12},{12,16},{16,20},{20,24},{24,28},{28,0},{1,5},{5... | collective-permute-start | bytes 6291464 | tf_op jit(solution)/shard_map/ppermute | solution.py:44
  138.8 1.3 copy-start.9
  140.1 25.6 %collective-permute-start.5 = (bf16[1024,1024]{1,0:T(8,128)(2,1)S(1)}, bf16[1024,1024]{1,0:T(8,128)(2,1)}, u32[]{:S(2)}, u32[]{:S(2)}) collective-permute-start(bf16[1024,1024]{1,0:T(8,128)(2,1)S(1)} %collective-permute-done.4), channel_id=1, source_target_pairs={{0,4},{4,8},{8,12},{12,16},{16,20},{20,24},{24,28},{28,0},{1,5},{5... | collective-permute-start | bytes 6291464 | tf_op jit(solution)/shard_map/ppermute | solution.py:44
  165.6 25.8 %collective-permute-start.6 = (bf16[1024,1024]{1,0:T(8,128)(2,1)}, bf16[1024,1024]{1,0:T(8,128)(2,1)}, u32[]{:S(2)}, u32[]{:S(2)}) collective-permute-start(bf16[1024,1024]{1,0:T(8,128)(2,1)} %collective-permute-done.5), channel_id=1, source_target_pairs={{0,4},{4,8},{8,12},{12,16},{16,20},{20,24},{24,28},{28,0},{1,5},{5... | collective-permute-start | bytes 6291464 | tf_op jit(solution)/shard_map/ppermute | solution.py:44
  172.6 25.1 %copy-start.10 = (bf16[1024,1024]{1,0:T(8,128)(2,1)S(1)}, bf16[1024,1024]{1,0:T(8,128)(2,1)}, u32[]{:S(2)}) copy-start(bf16[1024,1024]{1,0:T(8,128)(2,1)} %copy-done.9) | copy-start | bytes 6291460
  172.7 26.5 %copy-start.8 = (bf16[1024,1024]{1,0:T(8,128)(2,1)S(1)}, bf16[1024,1024]{1,0:T(8,128)(2,1)}, u32[]{:S(2)}) copy-start(bf16[1024,1024]{1,0:T(8,128)(2,1)} %copy-done.7) | copy-start | bytes 6291460
  176.1 24.7 %copy-start.6 = (bf16[1024,1024]{1,0:T(8,128)(2,1)S(1)}, bf16[1024,1024]{1,0:T(8,128)(2,1)}, u32[]{:S(2)}) copy-start(bf16[1024,1024]{1,0:T(8,128)(2,1)} %copy-done.5) | copy-start | bytes 6291460
  194.5 7.8 %copy-start.4 = (bf16[1024,1024]{1,0:T(8,128)(2,1)S(1)}, bf16[1024,1024]{1,0:T(8,128)(2,1)}, u32[]{:S(2)}) copy-start(bf16[1024,1024]{1,0:T(8,128)(2,1)} %copy-done.3) | copy-start | bytes 6291460
  199.2 6.1 copy-start.2
  216.0 6.0 copy-start.12
  237.0 8.7 %copy-start.13 = (f32[5120]{0:T(1024)S(1)}, f32[5120]{0:T(1024)}, u32[]{:S(2)}) copy-start(f32[5120]{0:T(1024)} %param.7) | copy-start | bytes 61444
  245.8 7.9 %copy-start = (f32[40,384,128]{1,2,0:T(8,128)S(1)}, f32[40,384,128]{1,2,0:T(8,128)}, u32[]{:S(2)}) copy-start(f32[40,384,128]{1,2,0:T(8,128)} %gather_fusion.1) | copy-start | bytes 23592964
  245.8 7.9 %copy-start.1 = (bf16[384,5120]{0,1:T(8,128)(2,1)S(1)}, bf16[384,5120]{0,1:T(8,128)(2,1)}, u32[]{:S(2)}) copy-start(bf16[384,5120]{0,1:T(8,128)(2,1)} %copy.13) | copy-start | bytes 11796484
  287.0 2.6 copy-start.11
  301.2 59.5 %copy-start.14 = (f32[1024]{0:T(1024)S(1)}, f32[1024]{0:T(1024)}, u32[]{:S(2)}) copy-start(f32[1024]{0:T(1024)} %param.8) | copy-start | bytes 12292
Sparse Core Ops, SparseCore 0:
  301.4 177.3 reduce-scatter.1
